TPU v7x, 32 devices: a whole 2x2x4 slice. The times are simulated.
32 devices in a mesh: orb: 8 (over y, x, core), walk: 4 (over z).
Axes of the slice: x: 2, y: 2, z: 4, core: 2. Of those that a mesh axis runs over, the one named last changes fastest.
Arguments:
- chol: bfloat16 [32, 2048, 2048], P(None, 'orb', 'walk'), may hold values from -6 to 6
- orbitals: bfloat16 [2048, 1024], replicated, may hold values from -0.125 to 0.125
- greens: bfloat16 [4, 1024, 2048], P('walk'), may hold values from -0.00390625 to 0.00390625
- shift: float32 [32], P('orb'), may hold values from -6 to 6
Outputs:
- force_bias: float32 [4, 32], P('walk', 'orb')
- rotated: bfloat16 [32, 1024, 2048], P('orb', None, 'walk')
All inputs are finite; a program needn't handle non-finite values.
Results may differ from a plain program's by a relative error of at most 0.007.
Values may be sent and summed in bfloat16 or wider, within the bound.
No kernel may reach another device: no remote copies, remote signals or barrier semaphores. Data moves between devices by JAX's collectives and lax.ppermute only.
A program may use at most 64 MiB of HBM per device.

v0:
```python
import functools

import jax
import jax.numpy as jnp
from jax import lax
from jax.experimental import pallas as pl
from jax.experimental.pallas import tpu as pltpu
from jax.sharding import PartitionSpec as P


MIB = 2**20


def tied(value, *after):
    return lax.optimization_barrier((value, *after))[0]


def params(mib):
    return pltpu.CompilerParams(vmem_limit_bytes=mib * MIB)


def chips(k):
    return (k >> 1).bit_count()


def cost(flops, moved):
    return pl.CostEstimate(flops=flops, bytes_accessed=moved, transcendentals=0)


def terms_kernel(place, chol_ref, *refs):
    product_refs, out_ref = refs[:-1], refs[-1]
    block = chol_ref[0].astype(jnp.float32)
    for w, product in enumerate(product_refs):
        out_ref[w, 0] = jnp.sum(product[...].astype(jnp.float32) * block, axis=0, keepdims=True)


def force_terms(chol, products, me, count):
    vectors, rows, columns = chol.shape
    walkers = len(products)
    whole = pl.BlockSpec((rows, columns), lambda v, place: (0, 0))
    return pl.pallas_call(
        terms_kernel,
        out_shape=jax.ShapeDtypeStruct((walkers, vectors, 1, columns), jnp.float32),
        grid_spec=pltpu.PrefetchScalarGridSpec(
            num_scalar_prefetch=1,
            grid=(vectors,),
            in_specs=[
                pl.BlockSpec(
                    (1, rows, columns),
                    lambda v, place: ((place[0] ^ (v // count)) * count + v % count, 0, 0),
                )
            ]
            + [whole] * walkers,
            out_specs=pl.BlockSpec((walkers, 1, 1, columns), lambda v, place: (0, v, 0, 0)),
        ),
        compiler_params=params(56),
        cost_estimate=cost(2 * walkers * chol.size, 2 * chol.size),
        name="terms",
    )(me, chol, *products)


def turn_kernel(place, source_ref, out_ref):
    out_ref[...] = source_ref[...].T


def turned(orbitals, owners, rows):
    occupied = orbitals.shape[1]
    blocks = owners.shape[0]
    return pl.pallas_call(
        turn_kernel,
        out_shape=jax.ShapeDtypeStruct((occupied, blocks * rows), orbitals.dtype),
        grid_spec=pltpu.PrefetchScalarGridSpec(
            num_scalar_prefetch=1,
            grid=(blocks,),
            in_specs=[pl.BlockSpec((rows, occupied), lambda k, place: (place[k], 0))],
            out_specs=pl.BlockSpec((occupied, rows), lambda k, place: (0, k)),
        ),
        compiler_params=params(8),
        cost_estimate=cost(blocks * rows * occupied * 300, 4 * blocks * rows * occupied),
        name="turn",
    )(owners, orbitals)


def near_kernel(lhs_ref, *refs):
    block_refs, out_ref, rhs = refs[:-2], refs[-2], refs[-1]
    rows = block_refs[0].shape[1]
    for k, block in enumerate(block_refs):
        rhs[k * rows : (k + 1) * rows, :] = block[0]
    out_ref[0] = jnp.dot(lhs_ref[...], rhs[...], preferred_element_type=jnp.float32)


def near_sum(lhs, blocks):
    count, rows, columns = blocks[0].shape
    occupied, depth = lhs.shape
    return pl.pallas_call(
        near_kernel,
        out_shape=jax.ShapeDtypeStruct((count, occupied, columns), jnp.float32),
        grid=(count,),
        in_specs=[pl.BlockSpec((occupied, depth), lambda g: (0, 0))]
        + [pl.BlockSpec((1, rows, columns), lambda g: (g, 0, 0))] * len(blocks),
        out_specs=pl.BlockSpec((1, occupied, columns), lambda g: (g, 0, 0)),
        scratch_shapes=[pltpu.VMEM((depth, columns), jnp.bfloat16)],
        compiler_params=params(24),
        cost_estimate=cost(2 * count * occupied * depth * columns, 4 * count * occupied * columns),
        name="near",
    )(lhs, *blocks)


def far_kernel(g, blocks, lhs_ref, near_ref, *refs):
    block_refs, (out_ref, rhs, held, sems) = refs[:blocks], refs[-4:]
    rows = block_refs[0].shape[1]
    for k, block in enumerate(block_refs):
        rhs[k * rows : (k + 1) * rows, :] = block[0]
    tiles = sems.shape[0]
    tile = held.shape[0] // tiles
    copies = []
    for t in range(tiles):
        part = pl.ds(t * tile, tile)
        total = near_ref[g, part, :] + jnp.dot(
            lhs_ref[part, :], rhs[...], preferred_element_type=jnp.float32
        )
        held[part, :] = total.astype(held.dtype)
        copy = pltpu.make_async_copy(held.at[part, :], out_ref.at[g, part, :], sems.at[t])
        copy.start()
        copies.append(copy)
    for copy in copies:
        copy.wait()


def far_sum(lhs, near, blocks, rotated, g):
    _, _, columns = blocks[0].shape
    occupied, depth = lhs.shape
    tiles = 4
    held = [] if rotated is None else [rotated]
    whole, left = pl.BlockSpec(memory_space=pltpu.VMEM), pl.BlockSpec(memory_space=pl.ANY)
    return pl.pallas_call(
        functools.partial(far_kernel, g, len(blocks)),
        out_shape=jax.ShapeDtypeStruct(near.shape, jnp.bfloat16),
        in_specs=[whole] * (2 + len(blocks)) + [left] * len(held),
        out_specs=left,
        scratch_shapes=[
            pltpu.VMEM((depth, columns), jnp.bfloat16),
            pltpu.VMEM((occupied, columns), jnp.bfloat16),
            pltpu.SemaphoreType.DMA((tiles,)),
        ],
        input_output_aliases={2 + len(blocks): 0} if held else {},
        compiler_params=params(16),
        cost_estimate=cost(2 * occupied * depth * columns, 4 * occupied * columns),
        name="far",
    )(lhs, near, *blocks, *held)


def local(owners, chol, orbitals, greens, shift):
    walkers = greens.shape[2] // chol.shape[2]
    count = chol.shape[0] // owners
    rows, columns = chol.shape[1:]
    me, mine = lax.axis_index("orb"), lax.axis_index("walk")
    near_offsets = sorted((k for k in range(1, owners) if chips(k) <= 1), key=lambda k: (chips(k) != 1, k & 1, k))
    far_offsets = [k for k in range(1, owners) if chips(k) > 1]
    first = [k for k in near_offsets if chips(k) and not k & 1]

    def swap(value, axis, k, size):
        return lax.ppermute(value, axis, [(i, i ^ k) for i in range(size)])

    def part(source, k, start=0, size=count):
        return lax.dynamic_slice_in_dim(source, (me ^ k) * count + start, size, 0)

    near = {}
    pieces = [part(chol, k) for k in first]
    for k, piece in zip(first, pieces):
        near[k] = swap(piece, "orb", k, owners)

    orbitals, greens, chol_next = tied((orbitals, greens, chol), *pieces)
    orbital_rows = lax.dynamic_slice_in_dim(orbitals, me * rows, rows, 0)
    products = jnp.dot(orbital_rows, greens[0], preferred_element_type=jnp.float32)
    products = products.astype(jnp.bfloat16)
    arrived = []
    for k in range(walkers):
        piece = lax.dynamic_slice_in_dim(products, (mine ^ k) * columns, columns, 1)
        arrived.append(swap(piece, "walk", k, walkers) if k else piece)

    chol_next = tied(chol_next, products)
    near[0] = part(chol_next, 0)
    pieces = {k: part(chol_next, k) for k in near_offsets if k not in near}
    for k, piece in pieces.items():
        near[k] = swap(piece, "orb", k, owners)
    far = {}
    chol_next = tied(chol_next, *pieces.values())
    for k in far_offsets:
        far[0, k] = swap(part(chol_next, k, 0, 1), "orb", k, owners)

    order = jnp.array([0] + near_offsets, jnp.int32) ^ me
    lhs_near = turned(orbitals, order, rows)
    lhs_far = turned(orbitals, jnp.array(far_offsets, jnp.int32) ^ me, rows)

    terms = force_terms(chol, arrived, jnp.stack([me, mine]).astype(jnp.int32), count)
    terms = terms.sum(axis=(2, 3))
    total = terms[0] + sum(swap(terms[k], "walk", k, walkers) for k in range(1, walkers))
    total = total.reshape(owners, count)
    even, odd = total[0::2], total[1::2]
    even = even + swap(odd, "orb", 1, owners)
    arrivals = [swap(even[k : k + 1], "orb", 2 * k, owners) for k in range(1, owners // 2)]

    chol_next = tied(chol_next, even)
    for g in range(1, count):
        for k in far_offsets:
            far[g, k] = swap(part(chol_next, k, g, 1), "orb", k, owners)

    partial = near_sum(lhs_near, [near[k] for k in [0] + near_offsets])
    arrivals = tied(arrivals, partial)
    force_bias = even[:1] + sum(arrivals) - shift[None, :]
    rotated = None
    for g in range(count):
        rotated = far_sum(lhs_far, partial, [far[g, k] for k in far_offsets], rotated, g)
    return force_bias, rotated


def solution(mesh):
    in_specs = (P(None, "orb", "walk"), P(), P("walk", None, None), P("orb"))
    out_specs = (P("walk", "orb"), P("orb", None, "walk"))
    owners = mesh.shape["orb"]

    def body(*args):
        return local(owners, *args)

    return jax.shard_map(body, mesh=mesh, in_specs=in_specs, out_specs=out_specs, check_vma=False)
```

profile of v0, /device:TPU:0, one launch (start us, length us, event | category | flops | bytes accessed | tf_op | source)
XLA Modules:
  0.0 172.1 jit_solution(9772649109765970359)
XLA Ops:
  0.7 3.0 %constant_dynamic-slice_fusion.16 = (bf16[4,256,512]{2,1,0:T(8,128)(2,1)}, bf16[4,256,512]{2,1,0:T(8,128)(2,1)}) fusion(bf16[32,256,512]{2,1,0:T(8,128)(2,1)} %chol_ref.1, s32[]{:T(128)S(6)} %select_n.58, s32[]{:T(128)S(6)} %select_n.57), kind=kLoop, calls=%fused_computation.21 | loop fusion | bytes 4194312 | tf_op jit(solution)/shard_map/dynamic_slice | solution.py:166
  3.7 3.6 %fusion.2 = bf16[256,2048]{1,0:T(8,128)(2,1)S(1)} fusion(bf16[1,1024,2048]{2,1,0:T(8,128)(2,1)} %param.8, bf16[2048,1024]{1,0:T(8,128)(2,1)} %source_ref.1, s32[]{:T(128)S(6)} %select_n.59), kind=kOutput, calls=%fused_computation.2 | convolution fusion | flops 1074266112 | bytes 5767172 | tf_op jit(solution)/shard_map/dot_general | solution.py:175
  8.3 3.1 %collective-permute-start = (bf16[256,512]{1,0:T(8,128)(2,1)}, bf16[256,512]{1,0:T(8,128)(2,1)}, u32[]{:S(2)}, u32[]{:S(2)}) collective-permute-start(bf16[256,512]{1,0:T(8,128)(2,1)} %get-tuple-element.36), channel_id=1, source_target_pairs={{0,1},{1,0},{2,3},{3,2},{4,5},{5,4},{6,7},{7,6},{8,9},{9,8},{10,11... | collective-permute-start | bytes 786440 | tf_op jit(solution)/shard_map/ppermute | solution.py:163
  11.3 2.6 %collective-permute-start.1 = (bf16[256,512]{1,0:T(8,128)(2,1)}, bf16[256,512]{1,0:T(8,128)(2,1)}, u32[]{:S(2)}, u32[]{:S(2)}) collective-permute-start(bf16[256,512]{1,0:T(8,128)(2,1)} %get-tuple-element.35), channel_id=1, source_target_pairs={{0,2},{1,3},{2,0},{3,1},{4,6},{5,7},{6,4},{7,5},{8,10},{9,11},{10,... | collective-permute-start | bytes 786440 | tf_op jit(solution)/shard_map/ppermute | solution.py:163
  13.9 3.9 %constant_dynamic-slice_fusion.8 = (bf16[4,256,512]{2,1,0:T(8,128)(2,1)}, bf16[4,256,512]{2,1,0:T(8,128)(2,1)}, bf16[4,256,512]{2,1,0:T(8,128)(2,1)}, bf16[4,256,512]{2,1,0:T(8,128)(2,1)S(1)}) fusion(bf16[32,256,512]{2,1,0:T(8,128)(2,1)} %chol_ref.1, s32[]{:T(128)S(6)} %select_n.67, s32[]{:T(128)S(6)} %select_n.66, s32[]{:T(128)S(6)} %select_n.65, ...), kind=kLoop, calls=%fused_computation.12 | loop fusion | bytes 8388624 | tf_op jit(solution)/shard_map/dynamic_slice | solution.py:166
  18.2 2.6 %collective-permute-start.13 = (bf16[4,256,512]{2,1,0:T(8,128)(2,1)}, bf16[4,256,512]{2,1,0:T(8,128)(2,1)S(1)}, u32[]{:S(2)}, u32[]{:S(2)}) collective-permute-start(bf16[4,256,512]{2,1,0:T(8,128)(2,1)} %get-tuple-element.29), channel_id=1, source_target_pairs={{0,20},{4,16},{8,28},{12,24},{16,4},{20,0},{24,12},{28,8},{1,21},{... | collective-permute-start | bytes 3145736 | tf_op jit(solution)/shard_map/ppermute | solution.py:163
  21.4 1.9 %constant_dynamic-slice_fusion = (bf16[1,256,512]{2,1,0:T(8,128)(2,1)}, bf16[1,256,512]{2,1,0:T(8,128)(2,1)}) fusion(bf16[32,256,512]{2,1,0:T(8,128)(2,1)} %chol_ref.1, s32[]{:T(128)S(6)} %select_n.75, s32[]{:T(128)S(6)} %select_n.74), kind=kLoop, calls=%fused_computation.4 | loop fusion | bytes 1048584 | tf_op jit(solution)/shard_map/dynamic_slice | solution.py:166
  23.3 9.7 %collective-permute-done.1.refs_2_ = bf16[256,512]{1,0:T(8,128)(2,1)} collective-permute-done((bf16[256,512]{1,0:T(8,128)(2,1)}, bf16[256,512]{1,0:T(8,128)(2,1)}, u32[]{:S(2)}, u32[]{:S(2)}) %collective-permute-start.1) | collective-permute-done | bytes 262176 | tf_op jit(solution)/shard_map/ppermute | solution.py:163
  33.0 19.8 %terms.1 = f32[4,32,1,512]{3,2,1,0:T(1,128)} custom-call(s32[2]{0:T(128)} %pad_add_fusion.place, bf16[32,256,512]{2,1,0:T(8,128)(2,1)} %chol_ref.1, bf16[256,512]{1,0:T(8,128)(2,1)} %get-tuple-element.37.refs_0_, bf16[256,512]{1,0:T(8,128)(2,1)} %collective-permute-done.refs_1_, bf16[256,512]{1,0:T(8,128)(2,1)} %collective-permute-done.1.refs_2_, ...), custom_call_target="tpu_custom_call" | custom-call | flops 33554432 | bytes 8388608 | tf_op jit(solution)/shard_map/terms/pallas_call | solution.py:41
  54.2 4.9 %collective-permute-start.3 = (f32[32]{0:T(128)S(1)}, f32[32]{0:T(128)S(1)}, u32[]{:S(2)}, u32[]{:S(2)}) collective-permute-start(f32[32]{0:T(128)S(1)} %get-tuple-element.43), channel_id=1, source_target_pairs={{0,1},{1,0},{2,3},{3,2},{4,5},{5,4},{6,7},{7,6},{8,9},{9,8},{10,11... | collective-permute-start | bytes 392 | tf_op jit(solution)/shard_map/ppermute | solution.py:163
  60.6 2.5 %collective-permute-start.5 = (f32[32]{0:T(128)S(1)}, f32[32]{0:T(128)S(1)}, u32[]{:S(2)}, u32[]{:S(2)}) collective-permute-start(f32[32]{0:T(128)S(1)} %get-tuple-element.42), channel_id=1, source_target_pairs={{0,3},{1,2},{2,1},{3,0},{4,7},{5,6},{6,5},{7,4},{8,11},{9,10},{10,... | collective-permute-start | bytes 392 | tf_op jit(solution)/shard_map/ppermute | solution.py:163
  63.5 2.4 %collective-permute-start.21 = (bf16[1,256,512]{2,1,0:T(8,128)(2,1)}, bf16[1,256,512]{2,1,0:T(8,128)(2,1)S(1)}, u32[]{:S(2)}, u32[]{:S(2)}) collective-permute-start(bf16[1,256,512]{2,1,0:T(8,128)(2,1)} %get-tuple-element.21), channel_id=1, source_target_pairs={{0,24},{4,28},{8,16},{12,20},{16,8},{20,12},{24,0},{28,4},{1,25},{... | collective-permute-start | bytes 786440 | tf_op jit(solution)/shard_map/ppermute | solution.py:163
  67.3 1.5 collective-permute-start.10
  68.8 2.2 %collective-permute-done.21.refs_0_ = bf16[1,256,512]{2,1,0:T(8,128)(2,1)S(1)} collective-permute-done((bf16[1,256,512]{2,1,0:T(8,128)(2,1)}, bf16[1,256,512]{2,1,0:T(8,128)(2,1)S(1)}, u32[]{:S(2)}, u32[]{:S(2)}) %collective-permute-start.21) | collective-permute-done | bytes 262176 | tf_op jit(solution)/shard_map/ppermute | solution.py:163
  71.0 1.5 collective-permute-start.7
  72.5 21.1 %collective-permute-done.7 = f32[1,4]{1,0:T(1,128)S(1)} collective-permute-done((f32[1,4]{1,0:T(1,128)S(1)}, f32[1,4]{1,0:T(1,128)S(1)}, u32[]{:S(2)}, u32[]{:S(2)}) %collective-permute-start.7) | collective-permute-done | bytes 48 | tf_op jit(solution)/shard_map/ppermute | solution.py:163
  94.4 2.8 %collective-permute-done.8 = f32[1,4]{1,0:T(1,128)S(1)} collective-permute-done((f32[1,4]{1,0:T(1,128)S(1)}, f32[1,4]{1,0:T(1,128)S(1)}, u32[]{:S(2)}, u32[]{:S(2)}) %collective-permute-start.8) | collective-permute-done | bytes 48 | tf_op jit(solution)/shard_map/ppermute | solution.py:163
  97.2 1.7 collective-permute-start.9
  98.8 2.8 %collective-permute-done.9 = f32[1,4]{1,0:T(1,128)S(1)} collective-permute-done((f32[1,4]{1,0:T(1,128)S(1)}, f32[1,4]{1,0:T(1,128)S(1)}, u32[]{:S(2)}, u32[]{:S(2)}) %collective-permute-start.9) | collective-permute-done | bytes 48 | tf_op jit(solution)/shard_map/ppermute | solution.py:163
  102.4 2.2 %copy-done = bf16[2048,1024]{1,0:T(8,128)(2,1)S(1)} copy-done((bf16[2048,1024]{1,0:T(8,128)(2,1)S(1)}, bf16[2048,1024]{1,0:T(8,128)(2,1)}, u32[]{:S(2)}) %copy-start) | copy-done | bytes 4194328
  106.8 2.0 %turn.2.lhs_ref = bf16[1024,1536]{1,0:T(8,128)(2,1)S(1)} custom-call(s32[6]{0:T(128)S(1)} %broadcast_xor_fusion.1.place, bf16[2048,1024]{1,0:T(8,128)(2,1)S(1)} %copy-done.1), custom_call_target="tpu_custom_call" | custom-call | flops 471859200 | bytes 6291456 | tf_op jit(solution)/shard_map/turn/pallas_call | solution.py:69
  108.7 1.5 constant_dynamic-slice_fusion.2
  110.4 2.3 %collective-permute-start.19 = (bf16[1,256,512]{2,1,0:T(8,128)(2,1)S(1)}, bf16[1,256,512]{2,1,0:T(8,128)(2,1)S(1)}, u32[]{:S(2)}, u32[]{:S(2)}) collective-permute-start(bf16[1,256,512]{2,1,0:T(8,128)(2,1)S(1)} %get-tuple-element.23), channel_id=1, source_target_pairs={{0,24},{4,28},{8,16},{12,20},{16,8},{20,12},{24,0},{28,4},{1,25},{... | collective-permute-start | bytes 786440 | tf_op jit(solution)/shard_map/ppermute | solution.py:163
  112.7 2.3 %collective-permute-start.20 = (bf16[1,256,512]{2,1,0:T(8,128)(2,1)S(1)}, bf16[1,256,512]{2,1,0:T(8,128)(2,1)S(1)}, u32[]{:S(2)}, u32[]{:S(2)}) collective-permute-start(bf16[1,256,512]{2,1,0:T(8,128)(2,1)S(1)} %get-tuple-element.22), channel_id=1, source_target_pairs={{0,28},{4,24},{8,20},{12,16},{16,12},{20,8},{24,4},{28,0},{1,29},{... | collective-permute-start | bytes 786440 | tf_op jit(solution)/shard_map/ppermute | solution.py:163
  115.7 30.9 %collective-permute-done.11.refs_2_ = bf16[4,256,512]{2,1,0:T(8,128)(2,1)} collective-permute-done((bf16[4,256,512]{2,1,0:T(8,128)(2,1)}, bf16[4,256,512]{2,1,0:T(8,128)(2,1)}, u32[]{:S(2)}, u32[]{:S(2)}) %collective-permute-start.11) | collective-permute-done | bytes 1048608 | tf_op jit(solution)/shard_map/ppermute | solution.py:163
  146.5 8.3 %near.1.near_ref = f32[4,1024,512]{2,1,0:T(8,128)S(1)} custom-call(bf16[1024,1536]{1,0:T(8,128)(2,1)S(1)} %turn.2.lhs_ref, bf16[4,256,512]{2,1,0:T(8,128)(2,1)S(1)} %get-tuple-element.31.refs_0_, bf16[4,256,512]{2,1,0:T(8,128)(2,1)} %collective-permute-done.10.refs_1_, bf16[4,256,512]{2,1,0:T(8,128)(2,1)} %collective-permute-done.11.refs_2_, ...), custom_call_target="tpu_custom_call" | custom-call | flops 6442450944 | bytes 8388608 | tf_op jit(solution)/shard_map/near/pallas_call | solution.py:95
  154.9 1.7 collective-permute-start.15
  158.0 2.4 %collective-permute-start.16 = (bf16[1,256,512]{2,1,0:T(8,128)(2,1)S(1)}, bf16[1,256,512]{2,1,0:T(8,128)(2,1)S(1)}, u32[]{:S(2)}, u32[]{:S(2)}) collective-permute-start(bf16[1,256,512]{2,1,0:T(8,128)(2,1)S(1)} %get-tuple-element.26), channel_id=1, source_target_pairs={{0,28},{4,24},{8,20},{12,16},{16,12},{20,8},{24,4},{28,0},{1,29},{... | collective-permute-start | bytes 786440 | tf_op jit(solution)/shard_map/ppermute | solution.py:163
  160.5 1.4 far.5.refs_2_
  162.0 1.5 far.6.refs_2_
  164.2 6.4 %collective-permute-done.16.refs_1_ = bf16[1,256,512]{2,1,0:T(8,128)(2,1)S(1)} collective-permute-done((bf16[1,256,512]{2,1,0:T(8,128)(2,1)S(1)}, bf16[1,256,512]{2,1,0:T(8,128)(2,1)S(1)}, u32[]{:S(2)}, u32[]{:S(2)}) %collective-permute-start.16) | collective-permute-done | bytes 262176 | tf_op jit(solution)/shard_map/ppermute | solution.py:163
  170.6 1.4 far.7
  (52 shorter events, 13.3 us)
Async XLA Ops:
  8.3 15.0 %collective-permute-start = (bf16[256,512]{1,0:T(8,128)(2,1)}, bf16[256,512]{1,0:T(8,128)(2,1)}, u32[]{:S(2)}, u32[]{:S(2)}) collective-permute-start(bf16[256,512]{1,0:T(8,128)(2,1)} %get-tuple-element.36), channel_id=1, source_target_pairs={{0,1},{1,0},{2,3},{3,2},{4,5},{5,4},{6,7},{7,6},{8,9},{9,8},{10,11... | collective-permute-start | bytes 786440 | tf_op jit(solution)/shard_map/ppermute | solution.py:163
  11.3 21.6 %collective-permute-start.1 = (bf16[256,512]{1,0:T(8,128)(2,1)}, bf16[256,512]{1,0:T(8,128)(2,1)}, u32[]{:S(2)}, u32[]{:S(2)}) collective-permute-start(bf16[256,512]{1,0:T(8,128)(2,1)} %get-tuple-element.35), channel_id=1, source_target_pairs={{0,2},{1,3},{2,0},{3,1},{4,6},{5,7},{6,4},{7,5},{8,10},{9,11},{10,... | collective-permute-start | bytes 786440 | tf_op jit(solution)/shard_map/ppermute | solution.py:163
  13.9 19.0 %collective-permute-start.2 = (bf16[256,512]{1,0:T(8,128)(2,1)S(1)}, bf16[256,512]{1,0:T(8,128)(2,1)}, u32[]{:S(2)}, u32[]{:S(2)}) collective-permute-start(bf16[256,512]{1,0:T(8,128)(2,1)S(1)} %get-tuple-element.34), channel_id=1, source_target_pairs={{0,3},{1,2},{2,1},{3,0},{4,7},{5,6},{6,5},{7,4},{8,11},{9,10},{10,... | collective-permute-start | bytes 786440 | tf_op jit(solution)/shard_map/ppermute | solution.py:163
  17.8 92.5 %collective-permute-start.12 = (bf16[4,256,512]{2,1,0:T(8,128)(2,1)}, bf16[4,256,512]{2,1,0:T(8,128)(2,1)S(1)}, u32[]{:S(2)}, u32[]{:S(2)}) collective-permute-start(bf16[4,256,512]{2,1,0:T(8,128)(2,1)} %get-tuple-element.30), channel_id=1, source_target_pairs={{0,12},{4,8},{8,4},{12,0},{16,28},{20,24},{24,20},{28,16},{1,13},{... | collective-permute-start | bytes 3145736 | tf_op jit(solution)/shard_map/ppermute | solution.py:163
  18.2 92.2 %collective-permute-start.13 = (bf16[4,256,512]{2,1,0:T(8,128)(2,1)}, bf16[4,256,512]{2,1,0:T(8,128)(2,1)S(1)}, u32[]{:S(2)}, u32[]{:S(2)}) collective-permute-start(bf16[4,256,512]{2,1,0:T(8,128)(2,1)} %get-tuple-element.29), channel_id=1, source_target_pairs={{0,20},{4,16},{8,28},{12,24},{16,4},{20,0},{24,12},{28,8},{1,21},{... | collective-permute-start | bytes 3145736 | tf_op jit(solution)/shard_map/ppermute | solution.py:163
  23.3 89.4 %collective-permute-start.14 = (bf16[4,256,512]{2,1,0:T(8,128)(2,1)}, bf16[4,256,512]{2,1,0:T(8,128)(2,1)}, u32[]{:S(2)}, u32[]{:S(2)}) collective-permute-start(bf16[4,256,512]{2,1,0:T(8,128)(2,1)} %get-tuple-element.28), channel_id=1, source_target_pairs={{0,4},{4,0},{8,12},{12,8},{16,20},{20,16},{24,28},{28,24},{1,5},{5... | collective-permute-start | bytes 3145736 | tf_op jit(solution)/shard_map/ppermute | solution.py:163
  33.0 69.4 %copy-start.5 = (s32[2]{0:T(128)S(1)}, s32[2]{0:T(128)}, u32[]{:S(2)}) copy-start(s32[2]{0:T(128)} %constant.49.clone) | copy-start | bytes 28
  52.8 52.9 %copy-start.4 = (s32[6]{0:T(128)S(1)}, s32[6]{0:T(128)}, u32[]{:S(2)}) copy-start(s32[6]{0:T(128)} %constant.48.clone) | copy-start | bytes 76
  54.2 6.4 %collective-permute-start.3 = (f32[32]{0:T(128)S(1)}, f32[32]{0:T(128)S(1)}, u32[]{:S(2)}, u32[]{:S(2)}) collective-permute-start(f32[32]{0:T(128)S(1)} %get-tuple-element.43), channel_id=1, source_target_pairs={{0,1},{1,0},{2,3},{3,2},{4,5},{5,4},{6,7},{7,6},{8,9},{9,8},{10,11... | collective-permute-start | bytes 392 | tf_op jit(solution)/shard_map/ppermute | solution.py:163
  59.0 4.5 %collective-permute-start.4 = (f32[32]{0:T(128)S(1)}, f32[32]{0:T(128)S(1)}, u32[]{:S(2)}, u32[]{:S(2)}) collective-permute-start(f32[32]{0:T(128)S(1)} %get-tuple-element.41), channel_id=1, source_target_pairs={{0,2},{1,3},{2,0},{3,1},{4,6},{5,7},{6,4},{7,5},{8,10},{9,11},{10,... | collective-permute-start | bytes 392 | tf_op jit(solution)/shard_map/ppermute | solution.py:163
  60.6 5.4 %collective-permute-start.5 = (f32[32]{0:T(128)S(1)}, f32[32]{0:T(128)S(1)}, u32[]{:S(2)}, u32[]{:S(2)}) collective-permute-start(f32[32]{0:T(128)S(1)} %get-tuple-element.42), channel_id=1, source_target_pairs={{0,3},{1,2},{2,1},{3,0},{4,7},{5,6},{6,5},{7,4},{8,11},{9,10},{10,... | collective-permute-start | bytes 392 | tf_op jit(solution)/shard_map/ppermute | solution.py:163
  63.5 7.5 %collective-permute-start.21 = (bf16[1,256,512]{2,1,0:T(8,128)(2,1)}, bf16[1,256,512]{2,1,0:T(8,128)(2,1)S(1)}, u32[]{:S(2)}, u32[]{:S(2)}) collective-permute-start(bf16[1,256,512]{2,1,0:T(8,128)(2,1)} %get-tuple-element.21), channel_id=1, source_target_pairs={{0,24},{4,28},{8,16},{12,20},{16,8},{20,12},{24,0},{28,4},{1,25},{... | collective-permute-start | bytes 786440 | tf_op jit(solution)/shard_map/ppermute | solution.py:163
  66.1 1.2 collective-permute-start.6
  67.3 47.7 %collective-permute-start.10 = (bf16[4,256,512]{2,1,0:T(8,128)(2,1)}, bf16[4,256,512]{2,1,0:T(8,128)(2,1)}, u32[]{:S(2)}, u32[]{:S(2)}) collective-permute-start(bf16[4,256,512]{2,1,0:T(8,128)(2,1)} %get-tuple-element.33), channel_id=1, source_target_pairs={{0,8},{4,12},{8,0},{12,4},{16,24},{20,28},{24,16},{28,20},{1,9},{5... | collective-permute-start | bytes 3145736 | tf_op jit(solution)/shard_map/ppermute | solution.py:163
  71.0 22.6 %collective-permute-start.7 = (f32[1,4]{1,0:T(1,128)S(1)}, f32[1,4]{1,0:T(1,128)S(1)}, u32[]{:S(2)}, u32[]{:S(2)}) collective-permute-start(f32[1,4]{1,0:T(1,128)S(1)} %get-tuple-element.40), channel_id=1, source_target_pairs={{0,8},{4,12},{8,0},{12,4},{16,24},{20,28},{24,16},{28,20},{1,9},{5... | collective-permute-start | bytes 56 | tf_op jit(solution)/shard_map/ppermute | solution.py:163
  93.6 3.6 %collective-permute-start.8 = (f32[1,4]{1,0:T(1,128)S(1)}, f32[1,4]{1,0:T(1,128)S(1)}, u32[]{:S(2)}, u32[]{:S(2)}) collective-permute-start(f32[1,4]{1,0:T(1,128)S(1)} %get-tuple-element.39), channel_id=1, source_target_pairs={{0,16},{4,20},{8,24},{12,28},{16,0},{20,4},{24,8},{28,12},{1,17},{... | collective-permute-start | bytes 56 | tf_op jit(solution)/shard_map/ppermute | solution.py:163
  97.2 4.5 %collective-permute-start.9 = (f32[1,4]{1,0:T(1,128)S(1)}, f32[1,4]{1,0:T(1,128)S(1)}, u32[]{:S(2)}, u32[]{:S(2)}) collective-permute-start(f32[1,4]{1,0:T(1,128)S(1)} %get-tuple-element.38), channel_id=1, source_target_pairs={{0,24},{4,28},{8,16},{12,20},{16,8},{20,12},{24,0},{28,4},{1,25},{... | collective-permute-start | bytes 56 | tf_op jit(solution)/shard_map/ppermute | solution.py:163
  101.7 44.9 %collective-permute-start.11 = (bf16[4,256,512]{2,1,0:T(8,128)(2,1)}, bf16[4,256,512]{2,1,0:T(8,128)(2,1)}, u32[]{:S(2)}, u32[]{:S(2)}) collective-permute-start(bf16[4,256,512]{2,1,0:T(8,128)(2,1)} %get-tuple-element.32), channel_id=1, source_target_pairs={{0,16},{4,20},{8,24},{12,28},{16,0},{20,4},{24,8},{28,12},{1,17},{... | collective-permute-start | bytes 3145736 | tf_op jit(solution)/shard_map/ppermute | solution.py:163
  102.4 2.2 %copy-start = (bf16[2048,1024]{1,0:T(8,128)(2,1)S(1)}, bf16[2048,1024]{1,0:T(8,128)(2,1)}, u32[]{:S(2)}) copy-start(bf16[2048,1024]{1,0:T(8,128)(2,1)} %source_ref.1) | copy-start | bytes 12582916
  104.6 2.2 %copy-start.1 = (bf16[2048,1024]{1,0:T(8,128)(2,1)S(1)}, bf16[2048,1024]{1,0:T(8,128)(2,1)}, u32[]{:S(2)}) copy-start(bf16[2048,1024]{1,0:T(8,128)(2,1)} %source_ref.1) | copy-start | bytes 12582916
  106.8 3.5 %copy-start.2 = (bf16[1,256,512]{2,1,0:T(8,128)(2,1)S(1)}, bf16[1,256,512]{2,1,0:T(8,128)(2,1)}, u32[]{:S(2)}) copy-start(bf16[1,256,512]{2,1,0:T(8,128)(2,1)} %get-tuple-element.20) | copy-start | bytes 786436
  110.3 44.6 %collective-permute-start.22 = (bf16[1,256,512]{2,1,0:T(8,128)(2,1)S(1)}, bf16[1,256,512]{2,1,0:T(8,128)(2,1)S(1)}, u32[]{:S(2)}, u32[]{:S(2)}) collective-permute-start(bf16[1,256,512]{2,1,0:T(8,128)(2,1)S(1)} %copy-done.2), channel_id=1, source_target_pairs={{0,28},{4,24},{8,20},{12,16},{16,12},{20,8},{24,4},{28,0},{1,29},{... | collective-permute-start | bytes 786440 | tf_op jit(solution)/shard_map/ppermute | solution.py:163
  110.4 47.6 %collective-permute-start.19 = (bf16[1,256,512]{2,1,0:T(8,128)(2,1)S(1)}, bf16[1,256,512]{2,1,0:T(8,128)(2,1)S(1)}, u32[]{:S(2)}, u32[]{:S(2)}) collective-permute-start(bf16[1,256,512]{2,1,0:T(8,128)(2,1)S(1)} %get-tuple-element.23), channel_id=1, source_target_pairs={{0,24},{4,28},{8,16},{12,20},{16,8},{20,12},{24,0},{28,4},{1,25},{... | collective-permute-start | bytes 786440 | tf_op jit(solution)/shard_map/ppermute | solution.py:163
  112.7 47.8 %collective-permute-start.20 = (bf16[1,256,512]{2,1,0:T(8,128)(2,1)S(1)}, bf16[1,256,512]{2,1,0:T(8,128)(2,1)S(1)}, u32[]{:S(2)}, u32[]{:S(2)}) collective-permute-start(bf16[1,256,512]{2,1,0:T(8,128)(2,1)S(1)} %get-tuple-element.22), channel_id=1, source_target_pairs={{0,28},{4,24},{8,20},{12,16},{16,12},{20,8},{24,4},{28,0},{1,29},{... | collective-permute-start | bytes 786440 | tf_op jit(solution)/shard_map/ppermute | solution.py:163
  115.0 47.0 %collective-permute-start.17 = (bf16[1,256,512]{2,1,0:T(8,128)(2,1)S(1)}, bf16[1,256,512]{2,1,0:T(8,128)(2,1)S(1)}, u32[]{:S(2)}, u32[]{:S(2)}) collective-permute-start(bf16[1,256,512]{2,1,0:T(8,128)(2,1)S(1)} %get-tuple-element.25), channel_id=1, source_target_pairs={{0,24},{4,28},{8,16},{12,20},{16,8},{20,12},{24,0},{28,4},{1,25},{... | collective-permute-start | bytes 786440 | tf_op jit(solution)/shard_map/ppermute | solution.py:163
  146.5 15.4 %collective-permute-start.18 = (bf16[1,256,512]{2,1,0:T(8,128)(2,1)S(1)}, bf16[1,256,512]{2,1,0:T(8,128)(2,1)S(1)}, u32[]{:S(2)}, u32[]{:S(2)}) collective-permute-start(bf16[1,256,512]{2,1,0:T(8,128)(2,1)S(1)} %get-tuple-element.24), channel_id=1, source_target_pairs={{0,28},{4,24},{8,20},{12,16},{16,12},{20,8},{24,4},{28,0},{1,29},{... | collective-permute-start | bytes 786440 | tf_op jit(solution)/shard_map/ppermute | solution.py:163
  154.9 9.4 %collective-permute-start.15 = (bf16[1,256,512]{2,1,0:T(8,128)(2,1)S(1)}, bf16[1,256,512]{2,1,0:T(8,128)(2,1)S(1)}, u32[]{:S(2)}, u32[]{:S(2)}) collective-permute-start(bf16[1,256,512]{2,1,0:T(8,128)(2,1)S(1)} %get-tuple-element.27), channel_id=1, source_target_pairs={{0,24},{4,28},{8,16},{12,20},{16,8},{20,12},{24,0},{28,4},{1,25},{... | collective-permute-start | bytes 786440 | tf_op jit(solution)/shard_map/ppermute | solution.py:163
  158.0 12.6 %collective-permute-start.16 = (bf16[1,256,512]{2,1,0:T(8,128)(2,1)S(1)}, bf16[1,256,512]{2,1,0:T(8,128)(2,1)S(1)}, u32[]{:S(2)}, u32[]{:S(2)}) collective-permute-start(bf16[1,256,512]{2,1,0:T(8,128)(2,1)S(1)} %get-tuple-element.26), channel_id=1, source_target_pairs={{0,28},{4,24},{8,20},{12,16},{16,12},{20,8},{24,4},{28,0},{1,29},{... | collective-permute-start | bytes 786440 | tf_op jit(solution)/shard_map/ppermute | solution.py:163
  161.9 1.5 copy-start.3
where the time goes:
time: 173 us; the launch traced here: 172 us
  waiting for transfers between devices  78.3 us (45%)
  Pallas kernels  36.9 us (21%)
  starting transfers between devices  35.1 us (20%)
  local copies, waits for them, and re-layouts  14.8 us (9%)
  matrix products  3.61 us (2%)
  other arithmetic  2.51 us (1%)
    ppermute x23, waiting for transfers between devices, swap(): return lax.ppermute(value, axis, [(i, i ^ k) for i in range(size)])  78.3 us
    ppermute x23, starting transfers between devices, swap(): return lax.ppermute(value, axis, [(i, i ^ k) for i in range(size)])  35.1 us
    pallas_call x1, Pallas kernels, force_terms(): pl.pallas_call(terms_kernel, out_shape=jax.ShapeDtypeStruct((walkers, vec...  19.8 us
    dynamic_slice x4, local copies, waits for them, and re-layouts, part(): return lax.dynamic_slice_in_dim(source, (me ^ k) * count + start, size, 0)  10.4 us
    pallas_call x1, Pallas kernels, near_sum(): pl.pallas_call(near_kernel, out_shape=jax.ShapeDtypeStruct((count, occupi...  8.3 us
    pallas_call x4, Pallas kernels, far_sum(): pl.pallas_call(functools.partial(far_kernel, g, len(blocks)), out_shape=j...  5.8 us
    dot_general x1, matrix products, local(): jnp.dot(orbital_rows, greens[0], preferred_element_type=jnp.float32)  3.61 us
  transfers between devices with their start and end apart: 23, of which 11 were waited for; matrix products, arithmetic and copies ran while one was open for 6% of the time, Pallas kernels for 21%

commit v1 on v0

v1 whole, which is shorter than its diff:
```python
import functools

import jax
import jax.numpy as jnp
from jax import lax
from jax.experimental import pallas as pl
from jax.experimental.pallas import tpu as pltpu
from jax.sharding import PartitionSpec as P


MIB = 2**20


def tied(value, *after):
    return lax.optimization_barrier((value, *after))[0]


def params(mib):
    return pltpu.CompilerParams(vmem_limit_bytes=mib * MIB)


def offsets(owners):
    chips = lambda k: (k >> 1).bit_count()
    first = [k for k in range(owners - 2, 0, -2) if chips(k) == 1]
    second = [k + 1 for k in first] + [1]
    return first, second, [k for k in range(1, owners) if chips(k) > 1]


def cost(flops, moved):
    return pl.CostEstimate(flops=flops, bytes_accessed=moved, transcendentals=0)


def terms_kernel(place, chol_ref, *refs):
    product_refs, out_ref = refs[:-1], refs[-1]
    for v in range(chol_ref.shape[0]):
        block = chol_ref[v].astype(jnp.float32)
        for w, product in enumerate(product_refs):
            terms = jnp.sum(product[...].astype(jnp.float32) * block, axis=0, keepdims=True)
            out_ref[w, v] = terms


def force_terms(chol, products, me, count):
    vectors, rows, columns = chol.shape
    walkers = len(products)
    whole = pl.BlockSpec((rows, columns), lambda v, place: (0, 0))
    return pl.pallas_call(
        terms_kernel,
        out_shape=jax.ShapeDtypeStruct((walkers, vectors, 1, columns), jnp.float32),
        grid_spec=pltpu.PrefetchScalarGridSpec(
            num_scalar_prefetch=1,
            grid=(vectors // count,),
            in_specs=[pl.BlockSpec((count, rows, columns), lambda v, place: (place[0] ^ v, 0, 0))]
            + [whole] * walkers,
            out_specs=pl.BlockSpec((walkers, count, 1, columns), lambda v, place: (0, v, 0, 0)),
        ),
        compiler_params=params(56),
        cost_estimate=cost(2 * walkers * chol.size, 2 * chol.size),
        name="terms",
    )(me, chol, *products)


def turn_kernel(place, source_ref, out_ref):
    out_ref[...] = source_ref[...].T


def turned(orbitals, owners, rows):
    occupied = orbitals.shape[1]
    blocks = owners.shape[0]
    return pl.pallas_call(
        turn_kernel,
        out_shape=jax.ShapeDtypeStruct((occupied, blocks * rows), orbitals.dtype),
        grid_spec=pltpu.PrefetchScalarGridSpec(
            num_scalar_prefetch=1,
            grid=(blocks,),
            in_specs=[pl.BlockSpec((rows, occupied), lambda k, place: (place[k], 0))],
            out_specs=pl.BlockSpec((occupied, rows), lambda k, place: (0, k)),
        ),
        compiler_params=params(8),
        cost_estimate=cost(blocks * rows * occupied * 300, 4 * blocks * rows * occupied),
        name="turn",
    )(owners, orbitals)


def near_kernel(counts, lhs_ref, *refs):
    piece_refs, out_ref, rhs = refs[:-2], refs[-2], refs[-1]
    rows = piece_refs[0].shape[1]
    vector = pl.program_id(0)
    piece_refs = iter(piece_refs)
    for k, pieces in enumerate(counts):
        at, start = pl.ds(k * rows, rows), 0
        for size in pieces:
            piece = next(piece_refs)

            @pl.when((vector >= start) & (vector < start + size))
            def _():
                rhs[at, :] = piece[0]

            start += size
    out_ref[0] = jnp.dot(lhs_ref[...], rhs[...], preferred_element_type=jnp.float32)


def near_sum(lhs, blocks):
    counts = [[piece.shape[0] for piece in pieces] for pieces in blocks]
    count, (_, rows, columns) = sum(counts[0]), blocks[0][0].shape
    occupied, depth = lhs.shape
    specs = [pl.BlockSpec((occupied, depth), lambda g: (0, 0))]
    for pieces in counts:
        start = 0
        for size in pieces:
            at = functools.partial(lambda start, size, g: (jnp.clip(g - start, 0, size - 1), 0, 0), start, size)
            specs.append(pl.BlockSpec((1, rows, columns), at))
            start += size
    return pl.pallas_call(
        functools.partial(near_kernel, counts),
        out_shape=jax.ShapeDtypeStruct((count, occupied, columns), jnp.float32),
        grid=(count,),
        in_specs=specs,
        out_specs=pl.BlockSpec((1, occupied, columns), lambda g: (g, 0, 0)),
        scratch_shapes=[pltpu.VMEM((depth, columns), jnp.bfloat16)],
        compiler_params=params(24),
        cost_estimate=cost(2 * count * occupied * depth * columns, 4 * count * occupied * columns),
        name="near",
    )(lhs, *(piece for pieces in blocks for piece in pieces))


def far_kernel(first, blocks, lhs_ref, near_ref, *refs):
    block_refs, (out_ref, rhs, held, sems) = refs[:blocks], refs[-4:]
    size, rows, _ = block_refs[0].shape
    tiles = sems.shape[1]
    tile = held.shape[1] // tiles
    copies = []
    for v in range(size):
        for k, block in enumerate(block_refs):
            rhs[v, k * rows : (k + 1) * rows, :] = block[v]
        for t in range(tiles):
            part = pl.ds(t * tile, tile)
            total = near_ref[first + v, part, :] + jnp.dot(
                lhs_ref[part, :], rhs[v], preferred_element_type=jnp.float32
            )
            held[v, part, :] = total.astype(held.dtype)
            copy = pltpu.make_async_copy(
                held.at[v, part, :], out_ref.at[first + v, part, :], sems.at[v, t]
            )
            copy.start()
            copies.append(copy)
    for copy in copies:
        copy.wait()


def far_sum(lhs, near, blocks, rotated, first):
    size, _, columns = blocks[0].shape
    occupied, depth = lhs.shape
    tiles = 4
    given = [] if rotated is None else [rotated]
    whole, left = pl.BlockSpec(memory_space=pltpu.VMEM), pl.BlockSpec(memory_space=pl.ANY)
    return pl.pallas_call(
        functools.partial(far_kernel, first, len(blocks)),
        out_shape=jax.ShapeDtypeStruct(near.shape, jnp.bfloat16),
        in_specs=[whole] * (2 + len(blocks)) + [left] * len(given),
        out_specs=left,
        scratch_shapes=[
            pltpu.VMEM((size, depth, columns), jnp.bfloat16),
            pltpu.VMEM((size, occupied, columns), jnp.bfloat16),
            pltpu.SemaphoreType.DMA((size, tiles)),
        ],
        input_output_aliases={2 + len(blocks): 0} if given else {},
        compiler_params=params(20),
        cost_estimate=cost(2 * size * occupied * depth * columns, 4 * size * occupied * columns),
        name="far",
    )(lhs, near, *blocks, *given)


def local(owners, chol, orbitals, greens, shift):
    walkers = greens.shape[2] // chol.shape[2]
    count = chol.shape[0] // owners
    rows, columns = chol.shape[1:]
    me, mine = lax.axis_index("orb"), lax.axis_index("walk")
    first, second, far_offsets = offsets(owners)

    def swap(value, axis, k, size):
        return lax.ppermute(value, axis, [(i, i ^ k) for i in range(size)])

    def part(source, k, start=0, stop=count):
        return lax.dynamic_slice_in_dim(source, (me ^ k) * count + start, stop - start, 0)

    source, near = chol, {k: [] for k in first}
    for start, stop in ((0, 1), (1, count)):
        pieces = [part(source, k, start, stop) for k in first]
        source, orbitals, greens = tied((source, orbitals, greens), *pieces)
        for k, piece in zip(first, pieces):
            near[k].append(swap(piece, "orb", k, owners))

    orbital_rows = lax.dynamic_slice_in_dim(orbitals, me * rows, rows, 0)
    products = jnp.dot(orbital_rows, greens[0], preferred_element_type=jnp.float32)
    products = products.astype(jnp.bfloat16)
    pieces = [
        lax.dynamic_slice_in_dim(products, (mine ^ k) * columns, columns, 1) for k in range(walkers)
    ]
    source = tied(source, *pieces)
    arrived = pieces[:1] + [swap(pieces[k], "walk", k, walkers) for k in range(1, walkers)]

    pieces = {k: part(source, k) for k in [0] + second}
    source = tied(source, *pieces.values())
    near[0] = [pieces[0]]
    for k in second:
        near[k] = [swap(pieces[k], "orb", k, owners)]

    cuts = [0, max(count - 2, 0), count - 1, count]
    cuts = [(a, b) for a, b in zip(cuts, cuts[1:]) if a < b]
    pieces = [part(source, k, *cuts[0]) for k in far_offsets]
    far = [[swap(piece, "orb", k, owners) for k, piece in zip(far_offsets, pieces)]]

    order = [0] + first + second
    lhs_near = turned(orbitals, jnp.array(order, jnp.int32) ^ me, rows)
    lhs_far = turned(orbitals, jnp.array(far_offsets, jnp.int32) ^ me, rows)

    terms = force_terms(chol, arrived, jnp.stack([me, mine]).astype(jnp.int32), count)
    terms = terms.sum(axis=(2, 3))
    total = terms[0] + sum(swap(terms[k], "walk", k, walkers) for k in range(1, walkers))
    total = total.reshape(owners, count)
    even = total[0::2] + swap(total[1::2], "orb", 1, owners)
    sums = [swap(even[k : k + 1], "orb", 2 * k, owners) for k in range(1, owners // 2)]

    source = tied(source, even)
    for cut in cuts[1:]:
        far.append([swap(part(source, k, *cut), "orb", k, owners) for k in far_offsets])

    partial = near_sum(lhs_near, [near[k] for k in order])
    sums = tied(sums, partial)
    force_bias = even[:1] + sum(sums) - shift[None, :]
    rotated = None
    for (start, _), blocks in zip(cuts, far):
        rotated = far_sum(lhs_far, partial, blocks, rotated, start)
    return force_bias, rotated


def solution(mesh):
    in_specs = (P(None, "orb", "walk"), P(), P("walk", None, None), P("orb"))
    out_specs = (P("walk", "orb"), P("orb", None, "walk"))
    owners = mesh.shape["orb"]

    def body(*args):
        return local(owners, *args)

    return jax.shard_map(body, mesh=mesh, in_specs=in_specs, out_specs=out_specs, check_vma=False)
```

time: 173 us -> 154 us (0.89)
  Pallas kernels: 36.9 us -> 25.5 us
  waiting for transfers between devices: 78.3 us -> 69.1 us
  local copies, waits for them, and re-layouts: 14.8 us -> 23 us
  starting transfers between devices: 35.1 us -> 28.1 us
    pallas_call x1, Pallas kernels: 19.8 us -> 8.62 us  [force_terms(): pl.pallas_call(terms_kernel, out_shape=jax.ShapeDtypeStruct((walkers, vec...]
    ppermute x23, waiting for transfers between devices: 78.3 us -> 69.1 us  [swap(): return lax.ppermute(value, axis, [(i, i ^ k) for i in range(size)])]
    ppermute x23, starting transfers between devices: 35.1 us -> 28.1 us  [swap(): return lax.ppermute(value, axis, [(i, i ^ k) for i in range(size)])]
    unnamed x12 -> x24, local copies, waits for them, and re-layouts: 3.33 us -> 9.92 us
    dynamic_slice x5 -> x6, local copies, waits for them, and re-layouts: 11.3 us -> 12.9 us  [the longest x5 12 us: part(): lax.dynamic_slice_in_dim(source, (me ^ k) * count + start, stop - start, 0)]
    pallas_call x5 -> x4, Pallas kernels: 14.1 us -> 13.8 us  [the longest x1 8.9 us: near_sum(): pl.pallas_call(functools.partial(near_kernel, counts), out_shape=jax.Shap...]
  transfers between devices with their start and end apart: 23 -> 23, of which waited for: 11 -> 13; matrix products, arithmetic and copies ran while one was open for 6% -> 11% of each run, Pallas kernels for 21% -> 16%
where the time goes in v1:
time: 154 us; the launch traced here: 153 us
  waiting for transfers between devices  69.1 us (45%)
  starting transfers between devices  28.1 us (18%)
  Pallas kernels  25.5 us (17%)
  local copies, waits for them, and re-layouts  23 us (15%)
  matrix products  3.61 us (2%)
  other arithmetic  2.53 us (2%)
    ppermute x23, waiting for transfers between devices, swap(): return lax.ppermute(value, axis, [(i, i ^ k) for i in range(size)])  69.1 us
    ppermute x23, starting transfers between devices, swap(): return lax.ppermute(value, axis, [(i, i ^ k) for i in range(size)])  28.1 us
    dynamic_slice x5, local copies, waits for them, and re-layouts, part(): lax.dynamic_slice_in_dim(source, (me ^ k) * count + start, stop - start, 0)  12 us
    unnamed x24, local copies, waits for them, and re-layouts  9.92 us
    pallas_call x1, Pallas kernels, near_sum(): pl.pallas_call(functools.partial(near_kernel, counts), out_shape=jax.Shap...  8.9 us
    pallas_call x1, Pallas kernels, force_terms(): pl.pallas_call(terms_kernel, out_shape=jax.ShapeDtypeStruct((walkers, vec...  8.62 us
    pallas_call x3, Pallas kernels, far_sum(): pl.pallas_call(functools.partial(far_kernel, first, len(blocks)), out_sha...  4.94 us
    dot_general x1, matrix products, local(): jnp.dot(orbital_rows, greens[0], preferred_element_type=jnp.float32)  3.61 us
  transfers between devices with their start and end apart: 23, of which 13 were waited for; matrix products, arithmetic and copies ran while one was open for 11% of the time, Pallas kernels for 16%

profile of v1, /device:TPU:0, one launch (start us, length us, event | category | flops | bytes accessed | tf_op | source)
XLA Modules:
  0.0 152.6 jit_solution(10898828974068812612)
XLA Ops:
  0.6 1.9 %constant_dynamic-slice_fusion.16 = (bf16[1,256,512]{2,1,0:T(8,128)(2,1)}, bf16[1,256,512]{2,1,0:T(8,128)(2,1)}) fusion(bf16[32,256,512]{2,1,0:T(8,128)(2,1)} %chol_ref.1, s32[]{:T(128)S(6)} %select_n.58, s32[]{:T(128)S(6)} %select_n.57), kind=kLoop, calls=%fused_computation.21 | loop fusion | bytes 1048584 | tf_op jit(solution)/shard_map/dynamic_slice | solution.py:184
  2.5 3.0 %collective-permute-start.10 = (bf16[1,256,512]{2,1,0:T(8,128)(2,1)}, bf16[1,256,512]{2,1,0:T(8,128)(2,1)S(1)}, u32[]{:S(2)}, u32[]{:S(2)}) collective-permute-start(bf16[1,256,512]{2,1,0:T(8,128)(2,1)} %get-tuple-element.39), channel_id=1, source_target_pairs={{0,16},{4,20},{8,24},{12,28},{16,0},{20,4},{24,8},{28,12},{1,17},{... | collective-permute-start | bytes 786440 | tf_op jit(solution)/shard_map/ppermute | solution.py:181
  5.5 1.5 collective-permute-start.12
  7.0 2.7 %constant_dynamic-slice_fusion.14 = (bf16[3,256,512]{2,1,0:T(8,128)(2,1)}, bf16[3,256,512]{2,1,0:T(8,128)(2,1)}) fusion(bf16[32,256,512]{2,1,0:T(8,128)(2,1)} %chol_ref.1, s32[]{:T(128)S(6)} %select_n.60, s32[]{:T(128)S(6)} %select_n.59), kind=kLoop, calls=%fused_computation.19 | loop fusion | bytes 3145736 | tf_op jit(solution)/shard_map/dynamic_slice | solution.py:184
  9.8 3.6 %fusion.2 = bf16[256,2048]{1,0:T(8,128)(2,1)S(1)} fusion(bf16[1,1024,2048]{2,1,0:T(8,128)(2,1)} %param.8, bf16[2048,1024]{1,0:T(8,128)(2,1)} %source_ref.1, s32[]{:T(128)S(6)} %select_n.61), kind=kOutput, calls=%fused_computation.2 | convolution fusion | flops 1074266112 | bytes 5767172 | tf_op jit(solution)/shard_map/dot_general | solution.py:194
  14.3 1.6 %collective-permute-start = (bf16[256,512]{1,0:T(8,128)(2,1)S(1)}, bf16[256,512]{1,0:T(8,128)(2,1)S(1)}, u32[]{:S(2)}, u32[]{:S(2)}) collective-permute-start(bf16[256,512]{1,0:T(8,128)(2,1)S(1)} %get-tuple-element.42), channel_id=1, source_target_pairs={{0,1},{1,0},{2,3},{3,2},{4,5},{5,4},{6,7},{7,6},{8,9},{9,8},{10,11... | collective-permute-start | bytes 786440 | tf_op jit(solution)/shard_map/ppermute | solution.py:181
  15.8 2.6 %collective-permute-start.1 = (bf16[256,512]{1,0:T(8,128)(2,1)}, bf16[256,512]{1,0:T(8,128)(2,1)S(1)}, u32[]{:S(2)}, u32[]{:S(2)}) collective-permute-start(bf16[256,512]{1,0:T(8,128)(2,1)} %get-tuple-element.41), channel_id=1, source_target_pairs={{0,2},{1,3},{2,0},{3,1},{4,6},{5,7},{6,4},{7,5},{8,10},{9,11},{10,... | collective-permute-start | bytes 786440 | tf_op jit(solution)/shard_map/ppermute | solution.py:181
  19.3 3.9 %constant_dynamic-slice_fusion.6 = (bf16[4,256,512]{2,1,0:T(8,128)(2,1)}, bf16[4,256,512]{2,1,0:T(8,128)(2,1)}, bf16[4,256,512]{2,1,0:T(8,128)(2,1)}, bf16[4,256,512]{2,1,0:T(8,128)(2,1)S(1)}) fusion(bf16[32,256,512]{2,1,0:T(8,128)(2,1)} %chol_ref.1, s32[]{:T(128)S(6)} %select_n.69, s32[]{:T(128)S(6)} %select_n.68, s32[]{:T(128)S(6)} %select_n.67, ...), kind=kLoop, calls=%fused_computation.10 | loop fusion | bytes 8388624 | tf_op jit(solution)/shard_map/dynamic_slice | solution.py:184
  23.1 3.1 %collective-permute-done.refs_1_ = bf16[256,512]{1,0:T(8,128)(2,1)S(1)} collective-permute-done((bf16[256,512]{1,0:T(8,128)(2,1)S(1)}, bf16[256,512]{1,0:T(8,128)(2,1)S(1)}, u32[]{:S(2)}, u32[]{:S(2)}) %collective-permute-start) | collective-permute-done | bytes 262176 | tf_op jit(solution)/shard_map/ppermute | solution.py:181
  26.3 11.1 %collective-permute-done.1.refs_2_ = bf16[256,512]{1,0:T(8,128)(2,1)S(1)} collective-permute-done((bf16[256,512]{1,0:T(8,128)(2,1)}, bf16[256,512]{1,0:T(8,128)(2,1)S(1)}, u32[]{:S(2)}, u32[]{:S(2)}) %collective-permute-start.1) | collective-permute-done | bytes 262176 | tf_op jit(solution)/shard_map/ppermute | solution.py:181
  38.8 8.6 %terms.1 = f32[4,32,1,512]{3,2,1,0:T(1,128)} custom-call(s32[2]{0:T(128)} %pad_add_fusion.place, bf16[32,256,512]{2,1,0:T(8,128)(2,1)} %chol_ref.1, bf16[256,512]{1,0:T(8,128)(2,1)} %get-tuple-element.43.refs_0_, bf16[256,512]{1,0:T(8,128)(2,1)} %copy-done.6, bf16[256,512]{1,0:T(8,128)(2,1)} %copy-done.7, bf16[256,512]{1,0:T(8,128)(2,1)} %copy-done.8), custom_call_target="tpu_custom_call" | custom-call | flops 33554432 | bytes 8388608 | tf_op jit(solution)/shard_map/terms/pallas_call | solution.py:46
  48.8 3.6 %collective-permute-start.3 = (f32[32]{0:T(128)S(1)}, f32[32]{0:T(128)S(1)}, u32[]{:S(2)}, u32[]{:S(2)}) collective-permute-start(f32[32]{0:T(128)S(1)} %get-tuple-element.49), channel_id=1, source_target_pairs={{0,1},{1,0},{2,3},{3,2},{4,5},{5,4},{6,7},{7,6},{8,9},{9,8},{10,11... | collective-permute-start | bytes 392 | tf_op jit(solution)/shard_map/ppermute | solution.py:181
  54.0 2.5 %collective-permute-start.5 = (f32[32]{0:T(128)S(1)}, f32[32]{0:T(128)S(1)}, u32[]{:S(2)}, u32[]{:S(2)}) collective-permute-start(f32[32]{0:T(128)S(1)} %get-tuple-element.48), channel_id=1, source_target_pairs={{0,3},{1,2},{2,1},{3,0},{4,7},{5,6},{6,5},{7,4},{8,11},{9,10},{10,... | collective-permute-start | bytes 392 | tf_op jit(solution)/shard_map/ppermute | solution.py:181
  56.9 2.4 %collective-permute-done.5 = f32[32]{0:T(128)S(1)} collective-permute-done((f32[32]{0:T(128)S(1)}, f32[32]{0:T(128)S(1)}, u32[]{:S(2)}, u32[]{:S(2)}) %collective-permute-start.5) | collective-permute-done | bytes 160 | tf_op jit(solution)/shard_map/ppermute | solution.py:181
  62.9 2.2 %copy-done = bf16[2048,1024]{1,0:T(8,128)(2,1)S(1)} copy-done((bf16[2048,1024]{1,0:T(8,128)(2,1)S(1)}, bf16[2048,1024]{1,0:T(8,128)(2,1)}, u32[]{:S(2)}) %copy-start) | copy-done | bytes 4194328
  67.2 2.0 %turn.2.lhs_ref = bf16[1024,1536]{1,0:T(8,128)(2,1)S(1)} custom-call(s32[6]{0:T(128)S(1)} %broadcast_xor_fusion.1.place, bf16[2048,1024]{1,0:T(8,128)(2,1)S(1)} %copy-done.1), custom_call_target="tpu_custom_call" | custom-call | flops 471859200 | bytes 6291456 | tf_op jit(solution)/shard_map/turn/pallas_call | solution.py:69
  69.2 1.7 %copy-done.2 = bf16[1024,1536]{1,0:T(8,128)(2,1)} copy-done((bf16[1024,1536]{1,0:T(8,128)(2,1)}, bf16[1024,1536]{1,0:T(8,128)(2,1)S(1)}, u32[]{:S(2)}) %copy-start.2) | copy-done | bytes 3145752
  70.9 2.3 %constant_dynamic-slice_fusion = (bf16[2,256,512]{2,1,0:T(8,128)(2,1)}, bf16[2,256,512]{2,1,0:T(8,128)(2,1)}) fusion(bf16[32,256,512]{2,1,0:T(8,128)(2,1)} %chol_ref.1, s32[]{:T(128)S(6)} %select_n.75, s32[]{:T(128)S(6)} %select_n.74), kind=kLoop, calls=%fused_computation.4 | loop fusion | bytes 2097160 | tf_op jit(solution)/shard_map/dynamic_slice | solution.py:184
  74.4 5.3 %collective-permute-done.11.refs_2_ = bf16[3,256,512]{2,1,0:T(8,128)(2,1)} collective-permute-done((bf16[3,256,512]{2,1,0:T(8,128)(2,1)}, bf16[3,256,512]{2,1,0:T(8,128)(2,1)}, u32[]{:S(2)}, u32[]{:S(2)}) %collective-permute-start.11) | collective-permute-done | bytes 786464 | tf_op jit(solution)/shard_map/ppermute | solution.py:181
  80.2 17.4 %collective-permute-done.13.refs_4_ = bf16[3,256,512]{2,1,0:T(8,128)(2,1)} collective-permute-done((bf16[3,256,512]{2,1,0:T(8,128)(2,1)}, bf16[3,256,512]{2,1,0:T(8,128)(2,1)}, u32[]{:S(2)}, u32[]{:S(2)}) %collective-permute-start.13) | collective-permute-done | bytes 786464 | tf_op jit(solution)/shard_map/ppermute | solution.py:181
  97.7 2.0 %collective-permute-start.22 = (bf16[2,256,512]{2,1,0:T(8,128)(2,1)}, bf16[2,256,512]{2,1,0:T(8,128)(2,1)S(1)}, u32[]{:S(2)}, u32[]{:S(2)}) collective-permute-start(bf16[2,256,512]{2,1,0:T(8,128)(2,1)} %get-tuple-element.26), channel_id=1, source_target_pairs={{0,28},{4,24},{8,20},{12,16},{16,12},{20,8},{24,4},{28,0},{1,29},{... | collective-permute-start | bytes 1572872 | tf_op jit(solution)/shard_map/ppermute | solution.py:181
  99.7 2.4 %collective-permute-start.19 = (bf16[1,256,512]{2,1,0:T(8,128)(2,1)S(1)}, bf16[1,256,512]{2,1,0:T(8,128)(2,1)S(1)}, u32[]{:S(2)}, u32[]{:S(2)}) collective-permute-start(bf16[1,256,512]{2,1,0:T(8,128)(2,1)S(1)} %get-tuple-element.29), channel_id=1, source_target_pairs={{0,24},{4,28},{8,16},{12,20},{16,8},{20,12},{24,0},{28,4},{1,25},{... | collective-permute-start | bytes 786440 | tf_op jit(solution)/shard_map/ppermute | solution.py:181
  102.8 1.9 %copy-done.3 = bf16[1024,1536]{1,0:T(8,128)(2,1)S(1)} copy-done((bf16[1024,1536]{1,0:T(8,128)(2,1)S(1)}, bf16[1024,1536]{1,0:T(8,128)(2,1)}, u32[]{:S(2)}) %copy-start.3) | copy-done | bytes 3145752
  105.6 8.9 %near.1.near_ref = f32[4,1024,512]{2,1,0:T(8,128)S(1)} custom-call(bf16[1024,1536]{1,0:T(8,128)(2,1)S(1)} %copy-done.3, bf16[4,256,512]{2,1,0:T(8,128)(2,1)S(1)} %get-tuple-element.35.refs_0_, bf16[1,256,512]{2,1,0:T(8,128)(2,1)S(1)} %collective-permute-done.10.refs_1_, bf16[3,256,512]{2,1,0:T(8,128)(2,1)} %collective-permute-done.11.refs_2_, ...), custom_call_target="tpu_custom_call" | custom-call | flops 6442450944 | bytes 8388608 | tf_op jit(solution)/shard_map/near/pallas_call | solution.py:113
  114.6 16.7 %collective-permute-done.7 = f32[1,4]{1,0:T(1,128)S(1)} collective-permute-done((f32[1,4]{1,0:T(1,128)S(1)}, f32[1,4]{1,0:T(1,128)S(1)}, u32[]{:S(2)}, u32[]{:S(2)}) %collective-permute-start.7) | collective-permute-done | bytes 48 | tf_op jit(solution)/shard_map/ppermute | solution.py:181
  131.8 3.1 %collective-permute-done.8 = f32[1,4]{1,0:T(1,128)S(1)} collective-permute-done((f32[1,4]{1,0:T(1,128)S(1)}, f32[1,4]{1,0:T(1,128)S(1)}, u32[]{:S(2)}, u32[]{:S(2)}) %collective-permute-start.8) | collective-permute-done | bytes 48 | tf_op jit(solution)/shard_map/ppermute | solution.py:181
  134.9 2.3 %collective-permute-start.9 = (f32[1,4]{1,0:T(1,128)S(1)}, f32[1,4]{1,0:T(1,128)S(1)}, u32[]{:S(2)}, u32[]{:S(2)}) collective-permute-start(f32[1,4]{1,0:T(1,128)S(1)} %get-tuple-element.44), channel_id=1, source_target_pairs={{0,24},{4,28},{8,16},{12,20},{16,8},{20,12},{24,0},{28,4},{1,25},{... | collective-permute-start | bytes 56 | tf_op jit(solution)/shard_map/ppermute | solution.py:181
  137.2 2.2 %collective-permute-done.9 = f32[1,4]{1,0:T(1,128)S(1)} collective-permute-done((f32[1,4]{1,0:T(1,128)S(1)}, f32[1,4]{1,0:T(1,128)S(1)}, u32[]{:S(2)}, u32[]{:S(2)}) %collective-permute-start.9) | collective-permute-done | bytes 48 | tf_op jit(solution)/shard_map/ppermute | solution.py:181
  139.3 2.3 %collective-permute-start.17 = (bf16[1,256,512]{2,1,0:T(8,128)(2,1)S(1)}, bf16[1,256,512]{2,1,0:T(8,128)(2,1)S(1)}, u32[]{:S(2)}, u32[]{:S(2)}) collective-permute-start(bf16[1,256,512]{2,1,0:T(8,128)(2,1)S(1)} %get-tuple-element.31), channel_id=1, source_target_pairs={{0,24},{4,28},{8,16},{12,20},{16,8},{20,12},{24,0},{28,4},{1,25},{... | collective-permute-start | bytes 786440 | tf_op jit(solution)/shard_map/ppermute | solution.py:181
  141.6 2.0 %far.3.refs_2_ = bf16[4,1024,512]{2,1,0:T(8,128)(2,1)} custom-call(bf16[1024,512]{1,0:T(8,128)(2,1)S(1)} %turn.3.lhs_ref, f32[4,1024,512]{2,1,0:T(8,128)S(1)} %near.1.near_ref, bf16[2,256,512]{2,1,0:T(8,128)(2,1)S(1)} %collective-permute-done.21.refs_0_, bf16[2,256,512]{2,1,0:T(8,128)(2,1)S(1)} %collective-permute-done.22.refs_1_), custom_call_target="tpu_custom_call" | custom-call | flops 1073741824 | bytes 4194304 | tf_op jit(solution)/shard_map/far/pallas_call | solution.py:156
  145.7 3.0 %collective-permute-done.17.refs_0_ = bf16[1,256,512]{2,1,0:T(8,128)(2,1)S(1)} collective-permute-done((bf16[1,256,512]{2,1,0:T(8,128)(2,1)S(1)}, bf16[1,256,512]{2,1,0:T(8,128)(2,1)S(1)}, u32[]{:S(2)}, u32[]{:S(2)}) %collective-permute-start.17) | collective-permute-done | bytes 262176 | tf_op jit(solution)/shard_map/ppermute | solution.py:181
  148.7 2.4 %collective-permute-done.18.refs_1_ = bf16[1,256,512]{2,1,0:T(8,128)(2,1)S(1)} collective-permute-done((bf16[1,256,512]{2,1,0:T(8,128)(2,1)S(1)}, bf16[1,256,512]{2,1,0:T(8,128)(2,1)S(1)}, u32[]{:S(2)}, u32[]{:S(2)}) %collective-permute-start.18) | collective-permute-done | bytes 262176 | tf_op jit(solution)/shard_map/ppermute | solution.py:181
  (64 shorter events, 19.6 us)
Async XLA Ops:
  2.5 56.9 %collective-permute-start.10 = (bf16[1,256,512]{2,1,0:T(8,128)(2,1)}, bf16[1,256,512]{2,1,0:T(8,128)(2,1)S(1)}, u32[]{:S(2)}, u32[]{:S(2)}) collective-permute-start(bf16[1,256,512]{2,1,0:T(8,128)(2,1)} %get-tuple-element.39), channel_id=1, source_target_pairs={{0,16},{4,20},{8,24},{12,28},{16,0},{20,4},{24,8},{28,12},{1,17},{... | collective-permute-start | bytes 786440 | tf_op jit(solution)/shard_map/ppermute | solution.py:181
  5.5 54.5 %collective-permute-start.12 = (bf16[1,256,512]{2,1,0:T(8,128)(2,1)}, bf16[1,256,512]{2,1,0:T(8,128)(2,1)S(1)}, u32[]{:S(2)}, u32[]{:S(2)}) collective-permute-start(bf16[1,256,512]{2,1,0:T(8,128)(2,1)} %get-tuple-element.38), channel_id=1, source_target_pairs={{0,8},{4,12},{8,0},{12,4},{16,24},{20,28},{24,16},{28,20},{1,9},{5... | collective-permute-start | bytes 786440 | tf_op jit(solution)/shard_map/ppermute | solution.py:181
  14.3 12.0 %collective-permute-start = (bf16[256,512]{1,0:T(8,128)(2,1)S(1)}, bf16[256,512]{1,0:T(8,128)(2,1)S(1)}, u32[]{:S(2)}, u32[]{:S(2)}) collective-permute-start(bf16[256,512]{1,0:T(8,128)(2,1)S(1)} %get-tuple-element.42), channel_id=1, source_target_pairs={{0,1},{1,0},{2,3},{3,2},{4,5},{5,4},{6,7},{7,6},{8,9},{9,8},{10,11... | collective-permute-start | bytes 786440 | tf_op jit(solution)/shard_map/ppermute | solution.py:181
  15.8 21.5 %collective-permute-start.1 = (bf16[256,512]{1,0:T(8,128)(2,1)}, bf16[256,512]{1,0:T(8,128)(2,1)S(1)}, u32[]{:S(2)}, u32[]{:S(2)}) collective-permute-start(bf16[256,512]{1,0:T(8,128)(2,1)} %get-tuple-element.41), channel_id=1, source_target_pairs={{0,2},{1,3},{2,0},{3,1},{4,6},{5,7},{6,4},{7,5},{8,10},{9,11},{10,... | collective-permute-start | bytes 786440 | tf_op jit(solution)/shard_map/ppermute | solution.py:181
  18.4 18.9 %collective-permute-start.2 = (bf16[256,512]{1,0:T(8,128)(2,1)}, bf16[256,512]{1,0:T(8,128)(2,1)S(1)}, u32[]{:S(2)}, u32[]{:S(2)}) collective-permute-start(bf16[256,512]{1,0:T(8,128)(2,1)} %get-tuple-element.40), channel_id=1, source_target_pairs={{0,3},{1,2},{2,1},{3,0},{4,7},{5,6},{6,5},{7,4},{8,11},{9,10},{10,... | collective-permute-start | bytes 786440 | tf_op jit(solution)/shard_map/ppermute | solution.py:181
  26.2 11.1 %copy-start.6 = (bf16[256,512]{1,0:T(8,128)(2,1)}, bf16[256,512]{1,0:T(8,128)(2,1)S(1)}, u32[]{:S(2)}) copy-start(bf16[256,512]{1,0:T(8,128)(2,1)S(1)} %collective-permute-done.refs_1_) | copy-start | bytes 786436
  26.3 34.7 %copy-start.11 = (s32[2]{0:T(128)S(1)}, s32[2]{0:T(128)}, u32[]{:S(2)}) copy-start(s32[2]{0:T(128)} %constant.49.clone) | copy-start | bytes 28
  26.3 73.4 %collective-permute-start.14 = (bf16[4,256,512]{2,1,0:T(8,128)(2,1)}, bf16[4,256,512]{2,1,0:T(8,128)(2,1)S(1)}, u32[]{:S(2)}, u32[]{:S(2)}) collective-permute-start(bf16[4,256,512]{2,1,0:T(8,128)(2,1)} %get-tuple-element.34), channel_id=1, source_target_pairs={{0,20},{4,16},{8,28},{12,24},{16,4},{20,0},{24,12},{28,8},{1,21},{... | collective-permute-start | bytes 3145736 | tf_op jit(solution)/shard_map/ppermute | solution.py:181
  47.4 18.7 %copy-start.10 = (s32[6]{0:T(128)S(1)}, s32[6]{0:T(128)}, u32[]{:S(2)}) copy-start(s32[6]{0:T(128)} %constant.48.clone) | copy-start | bytes 76
  48.8 5.2 %collective-permute-start.3 = (f32[32]{0:T(128)S(1)}, f32[32]{0:T(128)S(1)}, u32[]{:S(2)}, u32[]{:S(2)}) collective-permute-start(f32[32]{0:T(128)S(1)} %get-tuple-element.49), channel_id=1, source_target_pairs={{0,1},{1,0},{2,3},{3,2},{4,5},{5,4},{6,7},{7,6},{8,9},{9,8},{10,11... | collective-permute-start | bytes 392 | tf_op jit(solution)/shard_map/ppermute | solution.py:181
  52.4 4.5 %collective-permute-start.4 = (f32[32]{0:T(128)S(1)}, f32[32]{0:T(128)S(1)}, u32[]{:S(2)}, u32[]{:S(2)}) collective-permute-start(f32[32]{0:T(128)S(1)} %get-tuple-element.47), channel_id=1, source_target_pairs={{0,2},{1,3},{2,0},{3,1},{4,6},{5,7},{6,4},{7,5},{8,10},{9,11},{10,... | collective-permute-start | bytes 392 | tf_op jit(solution)/shard_map/ppermute | solution.py:181
  54.0 5.4 %collective-permute-start.5 = (f32[32]{0:T(128)S(1)}, f32[32]{0:T(128)S(1)}, u32[]{:S(2)}, u32[]{:S(2)}) collective-permute-start(f32[32]{0:T(128)S(1)} %get-tuple-element.48), channel_id=1, source_target_pairs={{0,3},{1,2},{2,1},{3,0},{4,7},{5,6},{6,5},{7,4},{8,11},{9,10},{10,... | collective-permute-start | bytes 392 | tf_op jit(solution)/shard_map/ppermute | solution.py:181
  56.9 45.2 %collective-permute-start.15 = (bf16[4,256,512]{2,1,0:T(8,128)(2,1)}, bf16[4,256,512]{2,1,0:T(8,128)(2,1)}, u32[]{:S(2)}, u32[]{:S(2)}) collective-permute-start(bf16[4,256,512]{2,1,0:T(8,128)(2,1)} %get-tuple-element.33), channel_id=1, source_target_pairs={{0,12},{4,8},{8,4},{12,0},{16,28},{20,24},{24,20},{28,16},{1,13},{... | collective-permute-start | bytes 3145736 | tf_op jit(solution)/shard_map/ppermute | solution.py:181
  59.3 43.1 %collective-permute-start.16 = (bf16[4,256,512]{2,1,0:T(8,128)(2,1)}, bf16[4,256,512]{2,1,0:T(8,128)(2,1)}, u32[]{:S(2)}, u32[]{:S(2)}) collective-permute-start(bf16[4,256,512]{2,1,0:T(8,128)(2,1)} %get-tuple-element.32), channel_id=1, source_target_pairs={{0,4},{4,0},{8,12},{12,8},{16,20},{20,16},{24,28},{28,24},{1,5},{5... | collective-permute-start | bytes 3145736 | tf_op jit(solution)/shard_map/ppermute | solution.py:181
  59.4 20.3 %collective-permute-start.11 = (bf16[3,256,512]{2,1,0:T(8,128)(2,1)}, bf16[3,256,512]{2,1,0:T(8,128)(2,1)}, u32[]{:S(2)}, u32[]{:S(2)}) collective-permute-start(bf16[3,256,512]{2,1,0:T(8,128)(2,1)} %get-tuple-element.37), channel_id=1, source_target_pairs={{0,16},{4,20},{8,24},{12,28},{16,0},{20,4},{24,8},{28,12},{1,17},{... | collective-permute-start | bytes 2359304 | tf_op jit(solution)/shard_map/ppermute | solution.py:181
  60.7 1.6 %collective-permute-start.6 = (f32[4,4]{1,0:T(4,128)S(1)}, f32[4,4]{1,0:T(4,128)S(1)}, u32[]{:S(2)}, u32[]{:S(2)}) collective-permute-start(f32[4,4]{1,0:T(4,128)S(1)} %slice.35), channel_id=1, source_target_pairs={{0,4},{4,0},{8,12},{12,8},{16,20},{20,16},{24,28},{28,24},{1,5},{5... | collective-permute-start | bytes 200 | tf_op jit(solution)/shard_map/ppermute | solution.py:181
  62.3 35.3 %collective-permute-start.13 = (bf16[3,256,512]{2,1,0:T(8,128)(2,1)}, bf16[3,256,512]{2,1,0:T(8,128)(2,1)}, u32[]{:S(2)}, u32[]{:S(2)}) collective-permute-start(bf16[3,256,512]{2,1,0:T(8,128)(2,1)} %get-tuple-element.36), channel_id=1, source_target_pairs={{0,8},{4,12},{8,0},{12,4},{16,24},{20,28},{24,16},{28,20},{1,9},{5... | collective-permute-start | bytes 2359304 | tf_op jit(solution)/shard_map/ppermute | solution.py:181
  62.9 2.2 %copy-start = (bf16[2048,1024]{1,0:T(8,128)(2,1)S(1)}, bf16[2048,1024]{1,0:T(8,128)(2,1)}, u32[]{:S(2)}) copy-start(bf16[2048,1024]{1,0:T(8,128)(2,1)} %source_ref.1) | copy-start | bytes 12582916
  65.0 2.2 %copy-start.1 = (bf16[2048,1024]{1,0:T(8,128)(2,1)S(1)}, bf16[2048,1024]{1,0:T(8,128)(2,1)}, u32[]{:S(2)}) copy-start(bf16[2048,1024]{1,0:T(8,128)(2,1)} %source_ref.1) | copy-start | bytes 12582916
  69.2 1.7 %copy-start.2 = (bf16[1024,1536]{1,0:T(8,128)(2,1)}, bf16[1024,1536]{1,0:T(8,128)(2,1)S(1)}, u32[]{:S(2)}) copy-start(bf16[1024,1536]{1,0:T(8,128)(2,1)S(1)} %turn.2.lhs_ref) | copy-start | bytes 9437188
  79.8 61.9 %collective-permute-start.21 = (bf16[2,256,512]{2,1,0:T(8,128)(2,1)}, bf16[2,256,512]{2,1,0:T(8,128)(2,1)S(1)}, u32[]{:S(2)}, u32[]{:S(2)}) collective-permute-start(bf16[2,256,512]{2,1,0:T(8,128)(2,1)} %get-tuple-element.27), channel_id=1, source_target_pairs={{0,24},{4,28},{8,16},{12,20},{16,8},{20,12},{24,0},{28,4},{1,25},{... | collective-permute-start | bytes 1572872 | tf_op jit(solution)/shard_map/ppermute | solution.py:181
  97.7 44.0 %collective-permute-start.22 = (bf16[2,256,512]{2,1,0:T(8,128)(2,1)}, bf16[2,256,512]{2,1,0:T(8,128)(2,1)S(1)}, u32[]{:S(2)}, u32[]{:S(2)}) collective-permute-start(bf16[2,256,512]{2,1,0:T(8,128)(2,1)} %get-tuple-element.26), channel_id=1, source_target_pairs={{0,28},{4,24},{8,20},{12,16},{16,12},{20,8},{24,4},{28,0},{1,29},{... | collective-permute-start | bytes 1572872 | tf_op jit(solution)/shard_map/ppermute | solution.py:181
  99.7 44.0 %collective-permute-start.19 = (bf16[1,256,512]{2,1,0:T(8,128)(2,1)S(1)}, bf16[1,256,512]{2,1,0:T(8,128)(2,1)S(1)}, u32[]{:S(2)}, u32[]{:S(2)}) collective-permute-start(bf16[1,256,512]{2,1,0:T(8,128)(2,1)S(1)} %get-tuple-element.29), channel_id=1, source_target_pairs={{0,24},{4,28},{8,16},{12,20},{16,8},{20,12},{24,0},{28,4},{1,25},{... | collective-permute-start | bytes 786440 | tf_op jit(solution)/shard_map/ppermute | solution.py:181
  102.0 41.7 %collective-permute-start.20 = (bf16[1,256,512]{2,1,0:T(8,128)(2,1)S(1)}, bf16[1,256,512]{2,1,0:T(8,128)(2,1)S(1)}, u32[]{:S(2)}, u32[]{:S(2)}) collective-permute-start(bf16[1,256,512]{2,1,0:T(8,128)(2,1)S(1)} %get-tuple-element.28), channel_id=1, source_target_pairs={{0,28},{4,24},{8,20},{12,16},{16,12},{20,8},{24,4},{28,0},{1,29},{... | collective-permute-start | bytes 786440 | tf_op jit(solution)/shard_map/ppermute | solution.py:181
  102.4 28.9 %collective-permute-start.7 = (f32[1,4]{1,0:T(1,128)S(1)}, f32[1,4]{1,0:T(1,128)S(1)}, u32[]{:S(2)}, u32[]{:S(2)}) collective-permute-start(f32[1,4]{1,0:T(1,128)S(1)} %get-tuple-element.46), channel_id=1, source_target_pairs={{0,8},{4,12},{8,0},{12,4},{16,24},{20,28},{24,16},{28,20},{1,9},{5... | collective-permute-start | bytes 56 | tf_op jit(solution)/shard_map/ppermute | solution.py:181
  102.8 1.9 %copy-start.3 = (bf16[1024,1536]{1,0:T(8,128)(2,1)S(1)}, bf16[1024,1536]{1,0:T(8,128)(2,1)}, u32[]{:S(2)}) copy-start(bf16[1024,1536]{1,0:T(8,128)(2,1)} %copy-done.2) | copy-start | bytes 9437188
  104.7 0.9 copy-start.5
  131.3 3.6 %collective-permute-start.8 = (f32[1,4]{1,0:T(1,128)S(1)}, f32[1,4]{1,0:T(1,128)S(1)}, u32[]{:S(2)}, u32[]{:S(2)}) collective-permute-start(f32[1,4]{1,0:T(1,128)S(1)} %get-tuple-element.45), channel_id=1, source_target_pairs={{0,16},{4,20},{8,24},{12,28},{16,0},{20,4},{24,8},{28,12},{1,17},{... | collective-permute-start | bytes 56 | tf_op jit(solution)/shard_map/ppermute | solution.py:181
  134.9 4.5 %collective-permute-start.9 = (f32[1,4]{1,0:T(1,128)S(1)}, f32[1,4]{1,0:T(1,128)S(1)}, u32[]{:S(2)}, u32[]{:S(2)}) collective-permute-start(f32[1,4]{1,0:T(1,128)S(1)} %get-tuple-element.44), channel_id=1, source_target_pairs={{0,24},{4,28},{8,16},{12,20},{16,8},{20,12},{24,0},{28,4},{1,25},{... | collective-permute-start | bytes 56 | tf_op jit(solution)/shard_map/ppermute | solution.py:181
  139.3 9.4 %collective-permute-start.17 = (bf16[1,256,512]{2,1,0:T(8,128)(2,1)S(1)}, bf16[1,256,512]{2,1,0:T(8,128)(2,1)S(1)}, u32[]{:S(2)}, u32[]{:S(2)}) collective-permute-start(bf16[1,256,512]{2,1,0:T(8,128)(2,1)S(1)} %get-tuple-element.31), channel_id=1, source_target_pairs={{0,24},{4,28},{8,16},{12,20},{16,8},{20,12},{24,0},{28,4},{1,25},{... | collective-permute-start | bytes 786440 | tf_op jit(solution)/shard_map/ppermute | solution.py:181
  141.6 9.5 %collective-permute-start.18 = (bf16[1,256,512]{2,1,0:T(8,128)(2,1)S(1)}, bf16[1,256,512]{2,1,0:T(8,128)(2,1)S(1)}, u32[]{:S(2)}, u32[]{:S(2)}) collective-permute-start(bf16[1,256,512]{2,1,0:T(8,128)(2,1)S(1)} %get-tuple-element.30), channel_id=1, source_target_pairs={{0,28},{4,24},{8,20},{12,16},{16,12},{20,8},{24,4},{28,0},{1,29},{... | collective-permute-start | bytes 786440 | tf_op jit(solution)/shard_map/ppermute | solution.py:181
  143.7 1.5 copy-start.9
  (3 other events, 2.1 us)
